TPU v7x, 8 devices: a whole 2x2x1 slice. The times are simulated.
8 devices in a mesh: dp: 1 (over z), tp: 8 (over y, x, core).
Axes of the slice: x: 2, y: 2, z: 1, core: 2. Of those that a mesh axis runs over, the one named last changes fastest.
Arguments:
- hidden: bfloat16 [768, 1536], P('dp')
- tokens: int32 [768], P('dp')
- embedding: bfloat16 [151936, 1536], P('tp')
- head_w: bfloat16 [1536, 151936], P(None, 'tp')
- h_norm: float32 [1536], replicated
- e_norm: float32 [1536], replicated
- f_norm: float32 [1536], replicated
- o_norm: float32 [1536], replicated
- proj_w: bfloat16 [3072, 1536], P(None, 'tp')
- w_gate: bfloat16 [1536, 8960], P(None, 'tp')
- w_up: bfloat16 [1536, 8960], P(None, 'tp')
- w_down: bfloat16 [8960, 1536], P('tp')
Outputs:
- output 1: bfloat16 [768, 1536], P('dp')
- output 2: float32 [768, 151936], P('dp', 'tp')
All inputs are finite; a program needn't handle non-finite values.
Results may differ from a plain program's by a relative error of at most 0.0111966.
Values are sent between devices in bfloat16 or wider.
A program may use at most 1 GiB of HBM per device.

v0:
```python
import jax
import jax.numpy as jnp
from jax import lax
from jax.sharding import PartitionSpec as P

NORM_EPS = 1e-6


def rms_norm(values, norm_gain):
    wide_vals = values.astype(jnp.float32)
    inv_rms = lax.rsqrt(jnp.mean(wide_vals * wide_vals, axis=-1, keepdims=True) + NORM_EPS)
    return wide_vals * inv_rms * norm_gain


def solution(mesh):
    def draft_step(hidden, tokens, embedding, head_w, h_norm, e_norm, f_norm, o_norm, proj_w, w_gate, w_up, w_down):
        tp_index = lax.axis_index("tp")
        vocab_local = embedding.shape[0]
        local_ids = tokens - tp_index * vocab_local
        owned_mask = (local_ids >= 0) & (local_ids < vocab_local)
        picked = jnp.take(embedding, jnp.clip(local_ids, 0, vocab_local - 1), axis=0)
        picked = jnp.where(owned_mask[:, None], picked, jnp.zeros_like(picked))
        emb_rows = lax.psum(picked, "tp")
        joined = jnp.concatenate([rms_norm(hidden, h_norm), rms_norm(emb_rows, e_norm)], axis=-1).astype(jnp.bfloat16)
        proj_cols = jnp.dot(joined, proj_w, preferred_element_type=jnp.float32).astype(jnp.bfloat16)
        proj_full = lax.all_gather(proj_cols, "tp", axis=1, tiled=True)
        normed = rms_norm(proj_full, f_norm).astype(jnp.bfloat16)
        gate_val = jnp.dot(normed, w_gate, preferred_element_type=jnp.float32)
        up_val = jnp.dot(normed, w_up, preferred_element_type=jnp.float32)
        act_val = (jax.nn.silu(gate_val) * up_val).astype(jnp.bfloat16)
        down_part = jnp.dot(act_val, w_down, preferred_element_type=jnp.float32)
        down_sum = lax.psum(down_part, "tp")
        new_u = (proj_full.astype(jnp.float32) + down_sum).astype(jnp.bfloat16)
        out_norm = rms_norm(new_u, o_norm).astype(jnp.bfloat16)
        logits = jnp.dot(out_norm, head_w, preferred_element_type=jnp.float32)
        row_max = lax.pmax(jnp.max(logits, axis=-1), "tp")
        shifted = logits - row_max[:, None]
        row_sum = lax.psum(jnp.sum(jnp.exp(shifted), axis=-1), "tp")
        return new_u, shifted - jnp.log(row_sum)[:, None]

    specs_in = (P("dp", None), P("dp"), P("tp", None), P(None, "tp"), P(None), P(None), P(None), P(None), P(None, "tp"), P(None, "tp"), P(None, "tp"), P("tp", None))
    specs_out = (P("dp", None), P("dp", "tp"))
    return jax.shard_map(draft_step, mesh=mesh, in_specs=specs_in, out_specs=specs_out, check_vma=False)
```

profile of v0, /device:TPU:0, one launch (start us, length us, event | category | flops | bytes accessed | tf_op | source)
XLA Modules:
  0.0 421.3 jit_solution(14822330420960529113)
XLA Ops:
  7.2 0.0 copy-start
  7.2 0.0 all-reduce.3.cloned.1.call-start
  7.2 0.8 compare_and_fusion
  8.1 57.7 %gather_fusion = bf16[768,1536]{1,0:T(8,128)(2,1)} fusion(bf16[18992,1536]{1,0:T(8,128)(2,1)} %param.14, s32[1024]{0:T(1024)S(1)} %pad_clamp_fusion), kind=kCustom, calls=%fused_computation | custom fusion | bytes 4721664 | tf_op jit(solution)/shard_map/jit(_take)/gather | solution.py:21
  65.8 3.4 select_select_fusion
  69.2 0.0 all-reduce.3.cloned.1.call-update
  69.3 0.0 all-gather.2.cloned.1.call-start
  69.3 0.0 copy-start.2
  69.3 2.3 fusion
  71.7 0.0 copy-start.8
  71.7 2.0 fusion.2
  73.7 45.8 %all-reduce.3.cloned.1.call-done = bf16[768,1536]{1,0:T(8,128)(2,1)} async-done(((bf16[768,1536]{1,0:T(8,128)(2,1)}), bf16[768,1536]{1,0:T(8,128)(2,1)}) %all-reduce.3.cloned.1.call-update) | async-done | bytes 2359312 | tf_op jit(solution)/shard_map/psum | solution.py:23
  119.5 2.3 fusion.3
  121.9 0.6 fusion.5
  122.5 0.1 copy-done.6
  122.6 0.3 copy-done.9
  122.9 2.4 fusion.22
  125.3 0.0 all-gather.2.cloned.1.call-update
  125.4 0.2 all-reduce.5.cloned.1.call-start
  125.6 22.3 %all-gather.2.cloned.1.call-done = bf16[768,1536]{0,1:T(8,128)(2,1)} async-done(((bf16[768,192]{0,1:T(8,128)(2,1)}), bf16[768,1536]{0,1:T(8,128)(2,1)}) %all-gather.2.cloned.1.call-update) | async-done | bytes 2359312 | tf_op jit(solution)/shard_map/all_gather | solution.py:26
  147.9 2.2 fusion.9
  150.1 7.4 %fusion.26 = f32[768,1120]{0,1:T(8,128)} fusion(bf16[1536,1120]{0,1:T(8,128)(2,1)} %param.21, bf16[768,1536]{0,1:T(8,128)(2,1)} %all-gather.2.cloned.1.call-done, f32[1536]{0:T(1024)S(1)} %copy-done.10, f32[768]{0:T(1024)S(1)} %add_rsqrt_fusion.1), kind=kOutput, calls=%fused_computation.37 | convolution fusion | flops 2647130112 | bytes 9249792 | tf_op jit(solution)/shard_map/dot_general | solution.py:28
  157.5 14.0 %fusion.25 = f32[768,1536]{0,1:T(8,128)} fusion(bf16[1120,1536]{1,0:T(8,128)(2,1)S(1)} %copy-done, bf16[1536,1120]{0,1:T(8,128)(2,1)} %param.22, f32[768,1120]{0,1:T(8,128)} %fusion.26, bf16[768,1536]{0,1:T(8,128)(2,1)} %all-gather.2.cloned.1.call-done, f32[1536]{0:T(1024)S(1)} %copy-done.10, f32[768]{0:T(1024)S(1)} %add_rsqrt_fusion.1), kind=kOutput, calls=%fused_computation.36 | convolution fusion | flops 5294702592 | bytes 17409024 | tf_op jit(solution)/shard_map/dot_general | solution.py:31
  171.5 0.0 all-reduce.5.cloned.1.call-update
  171.5 75.2 %all-reduce.5.cloned.1.call-done = f32[768,1536]{0,1:T(8,128)} async-done(((f32[768,1536]{0,1:T(8,128)}), f32[768,1536]{0,1:T(8,128)}) %all-reduce.5.cloned.1.call-update) | async-done | bytes 4718608 | tf_op jit(solution)/shard_map/psum | solution.py:32
  246.7 4.5 %fusion.6 = (f32[768]{0:T(1024)S(1)}, bf16[768,1536]{0,1:T(8,128)(2,1)}) fusion(f32[768,1536]{0,1:T(8,128)} %all-reduce.5.cloned.1.call-done, bf16[768,1536]{0,1:T(8,128)(2,1)S(1)} %copy-done.4), kind=kLoop, calls=%fused_computation.18 | loop fusion | flops 7077120 | bytes 9440256 | tf_op jit(solution)/shard_map/reduce_sum | solution.py:11
  251.2 4.6 %copy.15 = bf16[768,1536]{1,0:T(8,128)(2,1)} copy(bf16[768,1536]{0,1:T(8,128)(2,1)} %get-tuple-element.5) | data formatting | bytes 4718592
  255.8 54.6 %fusion.33 = (f32[768]{0:T(1024)S(1)}, f32[768,18992]{0,1:T(8,128)}) fusion(bf16[1536,18992]{0,1:T(8,128)(2,1)} %param.15, bf16[768,1536]{0,1:T(8,128)(2,1)S(1)} %copy-done.5, f32[1536]{0:T(1024)S(1)} %copy-done.11, f32[768]{0:T(1024)S(1)} %add_rsqrt_fusion), kind=kOutput, calls=%fused_computation.48 | convolution fusion | flops 44827054080 | bytes 119058432 | tf_op jit(solution)/shard_map/dot_general | solution.py:35
  310.4 22.3 %pmax.7 = f32[768]{0:T(1024)S(1)} all-reduce(f32[768]{0:T(1024)S(1)} %get-tuple-element.9), channel_id=1, replica_groups=mesh['dp'=1,'tp'=8] {'tp'}, use_global_device_ids=true, to_apply=%region_7.8 | all-reduce | flops 768 | bytes 6144 | tf_op jit(solution)/shard_map/pmax | solution.py:36
  332.7 18.6 %exponential_reduce_fusion = f32[768]{0:T(1024)S(1)} fusion(f32[768,18992]{0,1:T(8,128)} %get-tuple-element.10, f32[768]{0:T(1024)S(1)} %pmax.7), kind=kLoop, calls=%fused_computation.1 | loop fusion | flops 29170944 | bytes 58349568 | tf_op jit(solution)/shard_map/reduce_sum | solution.py:38
  351.3 23.9 %psum.23 = f32[768]{0:T(1024)S(1)} all-reduce(f32[768]{0:T(1024)S(1)} %exponential_reduce_fusion), channel_id=1, replica_groups=mesh['dp'=1,'tp'=8] {'tp'}, use_global_device_ids=true, to_apply=%region_9.10 | all-reduce | flops 768 | bytes 6144 | tf_op jit(solution)/shard_map/psum | solution.py:38
  375.2 39.6 %subtract_subtract_fusion = f32[768,18992]{0,1:T(8,128)} fusion(f32[768,18992]{0,1:T(8,128)} %get-tuple-element.10, f32[768]{0:T(1024)S(1)} %log.3, f32[768]{0:T(1024)S(1)} %pmax.7), kind=kLoop, calls=%fused_computation.2 | loop fusion | flops 29171712 | bytes 116692992 | tf_op jit(solution)/shard_map/sub | solution.py:39
  (25 shorter events, 0.1 us)
Async XLA Ops:
  7.2 150.4 %copy-start = (bf16[1120,1536]{1,0:T(8,128)(2,1)S(1)}, bf16[1120,1536]{1,0:T(8,128)(2,1)}, u32[]{:S(2)}) copy-start(bf16[1120,1536]{1,0:T(8,128)(2,1)} %param.23) | copy-start | bytes 10321924
  7.2 112.3 %all-reduce.3.cloned.1.call-start = ((), (), s32[]{:S(2)}) async-start(), calls=%async_computation | async-start | bytes 4718592 | tf_op jit(solution)/shard_map/psum | solution.py:23
  69.2 2.4 copy-start.7
  69.3 78.6 %all-gather.2.cloned.1.call-start = ((), (), s32[]{:S(2)}) async-start(), calls=%async_computation.1 | async-start | bytes 2654208 | tf_op jit(solution)/shard_map/all_gather | solution.py:26
  69.3 2.4 copy-start.2
  71.7 50.2 %copy-start.8 = (f32[1536]{0:T(1024)S(1)}, f32[1536]{0:T(1024)}, u32[]{:S(2)}) copy-start(f32[1536]{0:T(1024)} %param.17) | copy-start | bytes 18436
  119.5 2.4 copy-start.3
  119.5 3.1 copy-start.6
  119.5 3.4 copy-start.9
  122.9 27.2 %copy-start.10 = (f32[1536]{0:T(1024)S(1)}, f32[1536]{0:T(1024)}, u32[]{:S(2)}) copy-start(f32[1536]{0:T(1024)} %param.18) | copy-start | bytes 18436
  125.4 121.3 %all-reduce.5.cloned.1.call-start = ((), (), s32[]{:S(2)}) async-start(), calls=%async_computation.2 | async-start | bytes 9437184 | tf_op jit(solution)/shard_map/psum | solution.py:32
  171.5 75.2 %copy-start.4 = (bf16[768,1536]{0,1:T(8,128)(2,1)S(1)}, bf16[768,1536]{0,1:T(8,128)(2,1)}, u32[]{:S(2)}) copy-start(bf16[768,1536]{0,1:T(8,128)(2,1)} %all-gather.2.cloned.1.call-done) | copy-start | bytes 7077892
  251.2 4.6 %copy-start.5 = (bf16[768,1536]{0,1:T(8,128)(2,1)S(1)}, bf16[768,1536]{0,1:T(8,128)(2,1)}, u32[]{:S(2)}) copy-start(bf16[768,1536]{0,1:T(8,128)(2,1)} %get-tuple-element.5) | copy-start | bytes 7077892
  251.2 4.6 %copy-start.11 = (f32[1536]{0:T(1024)S(1)}, f32[1536]{0:T(1024)}, u32[]{:S(2)}) copy-start(f32[1536]{0:T(1024)} %param.19) | copy-start | bytes 18436
  375.2 39.6 %copy-start.1 = (bf16[1120,1536]{1,0:T(8,128)(2,1)S(1)}, bf16[1120,1536]{1,0:T(8,128)(2,1)}, u32[]{:S(2)}) copy-start(bf16[1120,1536]{1,0:T(8,128)(2,1)} %param.23) | copy-start | bytes 10321924
Sparse Core Ops, SparseCore 0:
  69.4 50.0 all-reduce.2
  125.5 22.3 all-gather.1
  171.6 75.0 all-reduce.4
where the time goes:
time: 422 us; the launch traced here: 421 us
  waiting for transfers between devices  143 us (34%)
  matrix products  78.4 us (19%)
  other arithmetic  76.5 us (18%)
  local copies, waits for them, and re-layouts  62.8 us (15%)
  blocking collectives  46.2 us (11%)
  between operations  13.9 us (3%)
    psum x1, waiting for transfers between devices, draft_step(): down_sum = lax.psum(down_part, 'tp')  75.2 us
    gather x1, local copies, waits for them, and re-layouts, draft_step(): jnp.take(embedding, jnp.clip(local_ids, 0, vocab_local - 1), axis=0)  57.7 us
    dot_general x1, matrix products, draft_step(): logits = jnp.dot(out_norm, head_w, preferred_element_type=jnp.float32)  54.6 us
    psum x1, waiting for transfers between devices, draft_step(): emb_rows = lax.psum(picked, 'tp')  45.8 us
    sub x1, other arithmetic, draft_step(): return (new_u, shifted - jnp.log(row_sum)[:, None])  39.6 us
    psum x1, blocking collectives, draft_step(): row_sum = lax.psum(jnp.sum(jnp.exp(shifted), axis=-1), 'tp')  23.9 us
    pmax x1, blocking collectives, draft_step(): row_max = lax.pmax(jnp.max(logits, axis=-1), 'tp')  22.3 us
    all_gather x1, waiting for transfers between devices, draft_step(): proj_full = lax.all_gather(proj_cols, 'tp', axis=1, tiled=True)  22.3 us
  transfers between devices with their start and end apart: 3, of which 3 were waited for; matrix products, arithmetic and copies ran while one was open for 1% of the time, Pallas kernels for 0%

commit v1 on v0

--- a/solution.py
+++ b/solution.py
@@ -1,15 +1,138 @@
+import functools
+
 import jax
 import jax.numpy as jnp
 from jax import lax
+from jax.experimental import pallas as pl
+from jax.experimental.pallas import tpu as pltpu
 from jax.sharding import PartitionSpec as P
 
 NORM_EPS = 1e-6
+MESH = pl.DeviceIdType.MESH
+TP = 8
+HEAD_TILE = 512
+FINISH_TILE = 512
 
 
 def rms_norm(values, norm_gain):
     wide_vals = values.astype(jnp.float32)
     inv_rms = lax.rsqrt(jnp.mean(wide_vals * wide_vals, axis=-1, keepdims=True) + NORM_EPS)
     return wide_vals * inv_rms * norm_gain
+
+
+def head_kernel(vocab, tile, o_ref, w_ref, z_ref, stats_ref, m_ref, s_ref):
+    step = pl.program_id(0)
+    steps = pl.num_programs(0)
+    rows = o_ref.shape[0]
+
+    @pl.when(step == 0)
+    def _():
+        m_ref[...] = jnp.full(m_ref.shape, -jnp.inf, jnp.float32)
+        s_ref[...] = jnp.zeros(s_ref.shape, jnp.float32)
+
+    def account(z):
+        groups = z.reshape(z.shape[0] // 8, 8, rows)
+        m_old = m_ref[...]
+        m_new = jnp.maximum(m_old, jnp.max(groups, axis=0))
+        m_ref[...] = m_new
+        s_ref[...] = s_ref[...] * jnp.exp(m_old - m_new) + jnp.sum(jnp.exp(groups - m_new[None]), axis=0)
+
+    def part(size):
+        z = lax.dot_general(w_ref[pl.ds(0, size), :], o_ref[...], (((1,), (1,)), ((), ())), preferred_element_type=jnp.float32)
+        z_ref[pl.ds(pl.multiple_of(step * tile, tile), size), :] = z
+        account(z)
+
+    @pl.when(step < steps - 1)
+    def _():
+        part(tile)
+
+    @pl.when(step == steps - 1)
+    def _():
+        part(vocab - (pl.cdiv(vocab, tile) - 1) * tile)
+        m_old = m_ref[...]
+        m_row = jnp.max(m_old, axis=0, keepdims=True)
+        s_row = jnp.sum(s_ref[...] * jnp.exp(m_old - m_row), axis=0, keepdims=True)
+        stats_ref[0:1, :] = m_row
+        stats_ref[1:2, :] = s_row
+
+
+def lse_kernel(stats_ref, lse_ref, all_ref, send_sem, recv_sem):
+    me = lax.axis_index("tp")
+    barrier = pltpu.get_barrier_semaphore()
+    for hop in range(1, TP):
+        pl.semaphore_signal(barrier, inc=1, device_id={"tp": lax.rem(me + hop, TP)}, device_id_type=MESH)
+    pl.semaphore_wait(barrier, TP - 1)
+    copies = []
+    for hop in range(1, TP):
+        copy = pltpu.make_async_remote_copy(
+            src_ref=stats_ref, dst_ref=all_ref.at[hop], send_sem=send_sem.at[hop], recv_sem=recv_sem.at[hop],
+            device_id={"tp": lax.rem(me + hop, TP)}, device_id_type=MESH)
+        copy.start()
+        copies.append(copy)
+    m = stats_ref[0:1, :]
+    for copy in copies:
+        copy.wait()
+    for hop in range(1, TP):
+        m = jnp.maximum(m, all_ref[hop, 0:1, :])
+    s = stats_ref[1:2, :] * jnp.exp(stats_ref[0:1, :] - m)
+    for hop in range(1, TP):
+        s = s + all_ref[hop, 1:2, :] * jnp.exp(all_ref[hop, 0:1, :] - m)
+    lse_ref[...] = jnp.broadcast_to(m + jnp.log(s), lse_ref.shape)
+
+
+def finish_kernel(z_ref, lse_ref, out_ref):
+    vocab = z_ref.shape[0]
+    tile = out_ref.shape[0]
+    step = pl.program_id(0)
+    last = pl.num_programs(0) - 1
+
+    def part(size):
+        start = pl.multiple_of(step * tile, tile)
+        out_ref[pl.ds(0, size), :] = z_ref[pl.ds(start, size), :] - lse_ref[0:1, :]
+
+    @pl.when(step < last)
+    def _():
+        part(tile)
+
+    @pl.when(step == last)
+    def _():
+        part(vocab - (pl.cdiv(vocab, tile) - 1) * tile)
+
+
+def head(out_norm, head_t):
+    rows, depth = out_norm.shape
+    vocab = head_t.shape[0]
+    steps = pl.cdiv(vocab, HEAD_TILE)
+    z, stats = pl.pallas_call(
+        functools.partial(head_kernel, vocab, HEAD_TILE),
+        grid=(steps,),
+        out_shape=(pltpu.VMEM((vocab, rows), jnp.float32), jax.ShapeDtypeStruct((2, rows), jnp.float32)),
+        in_specs=[pl.BlockSpec(memory_space=pltpu.VMEM), pl.BlockSpec((HEAD_TILE, depth), lambda i: (i, 0))],
+        out_specs=(pl.BlockSpec(memory_space=pltpu.VMEM), pl.BlockSpec(memory_space=pltpu.VMEM)),
+        scratch_shapes=[pltpu.VMEM((8, rows), jnp.float32)] * 2,
+        compiler_params=pltpu.CompilerParams(vmem_limit_bytes=7 * 2**20, dimension_semantics=("arbitrary",)),
+        name="head",
+    )(out_norm, head_t)
+    lse = pl.pallas_call(
+        lse_kernel,
+        out_shape=jax.ShapeDtypeStruct((8, rows), jnp.float32),
+        in_specs=[pl.BlockSpec(memory_space=pltpu.VMEM)],
+        out_specs=pl.BlockSpec(memory_space=pltpu.VMEM),
+        scratch_shapes=[pltpu.VMEM((TP, 2, rows), jnp.float32), pltpu.SemaphoreType.DMA((TP,)), pltpu.SemaphoreType.DMA((TP,))],
+        compiler_params=pltpu.CompilerParams(vmem_limit_bytes=2**20, collective_id=0, has_side_effects=True),
+        name="lse",
+    )(stats)
+    tile = FINISH_TILE
+    logp_t = pl.pallas_call(
+        finish_kernel,
+        grid=(pl.cdiv(vocab, tile),),
+        out_shape=jax.ShapeDtypeStruct((vocab, rows), jnp.float32),
+        in_specs=[pl.BlockSpec(memory_space=pltpu.VMEM)] * 2,
+        out_specs=pl.BlockSpec((tile, rows), lambda i: (i, 0)),
+        compiler_params=pltpu.CompilerParams(vmem_limit_bytes=5 * 2**20, dimension_semantics=("arbitrary",)),
+        name="finish",
+    )(pltpu.with_memory_space_constraint(z, pltpu.VMEM), lse)
+    return logp_t.T
 
 
 def solution(mesh):
@@ -32,11 +155,7 @@
         down_sum = lax.psum(down_part, "tp")
         new_u = (proj_full.astype(jnp.float32) + down_sum).astype(jnp.bfloat16)
         out_norm = rms_norm(new_u, o_norm).astype(jnp.bfloat16)
-        logits = jnp.dot(out_norm, head_w, preferred_element_type=jnp.float32)
-        row_max = lax.pmax(jnp.max(logits, axis=-1), "tp")
-        shifted = logits - row_max[:, None]
-        row_sum = lax.psum(jnp.sum(jnp.exp(shifted), axis=-1), "tp")
-        return new_u, shifted - jnp.log(row_sum)[:, None]
+        return new_u, head(out_norm, head_w.T)
 
     specs_in = (P("dp", None), P("dp"), P("tp", None), P(None, "tp"), P(None), P(None), P(None), P(None), P(None, "tp"), P(None, "tp"), P(None, "tp"), P("tp", None))
     specs_out = (P("dp", None), P("dp", "tp"))

time: 422 us -> 357 us (0.85)
  Pallas kernels: 0 us -> 93 us
  other arithmetic: 76.5 us -> 15.7 us
  matrix products: 78.4 us -> 26.6 us
  blocking collectives: 46.2 us -> 0 us
    pallas_call x0 -> x3, Pallas kernels: none -> 93 us  [the longest x1 63.4 us: head(): pl.pallas_call(functools.partial(head_kernel, vocab, HEAD_TILE), grid=(st...]
    dot_general x1 -> x0, matrix products: 54.6 us -> none  [draft_step(): logits = jnp.dot(out_norm, head_w, preferred_element_type=jnp.float32)]
    sub x1 -> x0, other arithmetic: 39.6 us -> none  [draft_step(): return (new_u, shifted - jnp.log(row_sum)[:, None])]
    psum x1 -> x0, blocking collectives: 23.9 us -> none  [draft_step(): row_sum = lax.psum(jnp.sum(jnp.exp(shifted), axis=-1), 'tp')]
    pmax x1 -> x0, blocking collectives: 22.3 us -> none  [draft_step(): row_max = lax.pmax(jnp.max(logits, axis=-1), 'tp')]
    reduce_sum x1 -> x0, other arithmetic: 18.6 us -> none  [draft_step(): row_sum = lax.psum(jnp.sum(jnp.exp(shifted), axis=-1), 'tp')]
    reduce_sum x4, other arithmetic: 11.3 us -> 6.49 us  [rms_norm(): jnp.mean(wide_vals * wide_vals, axis=-1, keepdims=True) + NORM_EPS]
where the time goes in v1:
time: 357 us
  waiting for transfers between devices  146 us (41%)
  Pallas kernels  93 us (26%)
  local copies, waits for them, and re-layouts  61.9 us (17%)
  matrix products  26.6 us (7%)
  other arithmetic  15.7 us (4%)
  between operations  13.9 us (4%)
    psum x1, waiting for transfers between devices, draft_step(): down_sum = lax.psum(down_part, 'tp')  75.2 us
    pallas_call x1, Pallas kernels, head(): pl.pallas_call(functools.partial(head_kernel, vocab, HEAD_TILE), grid=(st...  63.4 us
    gather x1, local copies, waits for them, and re-layouts, draft_step(): jnp.take(embedding, jnp.clip(local_ids, 0, vocab_local - 1), axis=0)  57.4 us
    psum x1, waiting for transfers between devices, draft_step(): emb_rows = lax.psum(picked, 'tp')  48.2 us
    pallas_call x1, Pallas kernels, head(): pl.pallas_call(finish_kernel, grid=(pl.cdiv(vocab, tile),), out_shape=jax...  24.7 us
    all_gather x1, waiting for transfers between devices, draft_step(): proj_full = lax.all_gather(proj_cols, 'tp', axis=1, tiled=True)  22.5 us
    dot_general x1, matrix products, draft_step(): down_part = jnp.dot(act_val, w_down, preferred_element_type=jnp.float32)  17.6 us
  transfers between devices with their start and end apart: 3, of which 3 were waited for; matrix products, arithmetic and copies ran while one was open for 1% of the time, Pallas kernels for 0%

profile of v1, /device:TPU:0, one launch (start us, length us, event | category | flops | bytes accessed | tf_op | source)
XLA Modules:
  0.0 357.1 jit_solution(4497494021031453538)
XLA Ops:
  7.2 0.0 copy-start
  7.2 0.0 all-reduce.3.cloned.1.call-start
  7.2 0.8 compare_and_fusion
  8.0 57.4 %gather_fusion = bf16[768,1536]{1,0:T(8,128)(2,1)} fusion(bf16[18992,1536]{1,0:T(8,128)(2,1)} %param.14, s32[1024]{0:T(1024)S(1)} %pad_clamp_fusion), kind=kCustom, calls=%fused_computation | custom fusion | bytes 4721664 | tf_op jit(solution)/shard_map/jit(_take)/gather | solution.py:144
  65.4 3.6 %select_select_fusion = bf16[768,1536]{1,0:T(8,128)(2,1)} fusion(bf16[768,1536]{1,0:T(8,128)(2,1)} %gather_fusion, pred[768]{0:T(1024)(128)(4,1)S(1)} %get-tuple-element.8, pred[768]{0:T(1024)(128)(4,1)S(1)} %get-tuple-element.10), kind=kLoop, calls=%fused_computation.29 | loop fusion | flops 2359296 | bytes 4720128 | tf_op jit(solution)/shard_map/jit(_where)/select_n | solution.py:145
  69.0 0.0 all-reduce.3.cloned.1.call-update
  69.0 0.0 all-gather.2.cloned.1.call-start
  69.1 0.5 fusion
  69.6 0.1 copy-done.8
  69.7 2.0 fusion.2
  71.7 48.2 %all-reduce.3.cloned.1.call-done = bf16[768,1536]{1,0:T(8,128)(2,1)} async-done(((bf16[768,1536]{1,0:T(8,128)(2,1)}), bf16[768,1536]{1,0:T(8,128)(2,1)}) %all-reduce.3.cloned.1.call-update) | async-done | bytes 2359312 | tf_op jit(solution)/shard_map/psum | solution.py:146
  119.9 2.3 fusion.3
  122.3 0.0 copy-done.5
  122.3 0.6 fusion.5
  122.9 0.1 copy-done.7
  123.0 2.4 fusion.18
  125.4 0.0 all-gather.2.cloned.1.call-update
  125.5 0.0 all-reduce.5.cloned.1.call-start
  125.5 22.5 %all-gather.2.cloned.1.call-done = bf16[768,1536]{0,1:T(8,128)(2,1)} async-done(((bf16[768,192]{0,1:T(8,128)(2,1)}), bf16[768,1536]{0,1:T(8,128)(2,1)}) %all-gather.2.cloned.1.call-update) | async-done | bytes 2359312 | tf_op jit(solution)/shard_map/all_gather | solution.py:149
  148.0 3.0 copy.15
  151.0 0.5 fusion.9
  151.5 6.7 %fusion.24 = f32[768,1120]{0,1:T(8,128)} fusion(bf16[1536,1120]{0,1:T(8,128)(2,1)} %param.21, bf16[768,1536]{1,0:T(8,128)(2,1)S(1)} %copy.15, f32[1536]{0:T(1024)S(1)} %copy-done.11, f32[768]{0:T(1024)S(1)} %add_rsqrt_fusion.1), kind=kOutput, calls=%fused_computation.32 | convolution fusion | flops 2647130112 | bytes 9249792 | tf_op jit(solution)/shard_map/dot_general | solution.py:151
  158.2 17.6 %fusion.21 = f32[768,1536]{1,0:T(8,128)} fusion(bf16[1120,1536]{1,0:T(8,128)(2,1)} %param.23, bf16[1536,1120]{0,1:T(8,128)(2,1)} %param.22, f32[768,1120]{0,1:T(8,128)} %fusion.24, bf16[768,1536]{1,0:T(8,128)(2,1)S(1)} %copy.15, f32[1536]{0:T(1024)S(1)} %copy-done.11, f32[768]{0:T(1024)S(1)} %add_rsqrt_fusion.1), kind=kOutput, calls=%fused_computation.31 | convolution fusion | flops 5294702592 | bytes 17409024 | tf_op jit(solution)/shard_map/dot_general | solution.py:154
  175.8 0.0 all-reduce.5.cloned.1.call-update
  175.8 75.2 %all-reduce.5.cloned.1.call-done = f32[768,1536]{1,0:T(8,128)} async-done(((f32[768,1536]{1,0:T(8,128)}), f32[768,1536]{1,0:T(8,128)}) %all-reduce.5.cloned.1.call-update) | async-done | bytes 4718608 | tf_op jit(solution)/shard_map/psum | solution.py:155
  251.0 3.1 fusion.6
  254.1 2.1 fusion.8.o_ref
  256.3 63.4 %head.1 = (f32[18992,768]{1,0:T(8,128)S(1)}, f32[2,768]{1,0:T(2,128)}) custom-call(bf16[768,1536]{1,0:T(8,128)(2,1)} %fusion.8.o_ref, bf16[18992,1536]{1,0:T(8,128)(2,1)} %bitcast.6), custom_call_target="tpu_custom_call" | custom-call | tf_op jit(solution)/shard_map/head/pallas_call | solution.py:106
  319.7 0.7 copy-done.3
  320.4 4.9 %lse.1.lse_ref = f32[8,768]{1,0:T(8,128)S(1)} custom-call(f32[2,768]{1,0:T(2,128)S(1)} %copy-done.3), custom_call_target="tpu_custom_call" | custom-call | tf_op jit(solution)/shard_map/lse/pallas_call | solution.py:116
  325.3 0.6 copy-done.2
  325.9 24.7 %finish.1 = f32[18992,768]{1,0:T(8,128)} custom-call(f32[18992,768]{1,0:T(8,128)S(1)} %get-tuple-element.4.z_ref, f32[8,768]{1,0:T(8,128)} %copy-done.2), custom_call_target="tpu_custom_call" | custom-call | tf_op jit(solution)/shard_map/finish/pallas_call | solution.py:126
  (23 shorter events, 0.1 us)
Async XLA Ops:
  7.2 115.8 %copy-start = (bf16[3072,192]{0,1:T(8,128)(2,1)S(1)}, bf16[3072,192]{0,1:T(8,128)(2,1)}, u32[]{:S(2)}) copy-start(bf16[3072,192]{0,1:T(8,128)(2,1)} %param.20) | copy-start | bytes 3538948
  7.2 112.7 %all-reduce.3.cloned.1.call-start = ((), (), s32[]{:S(2)}) async-start(), calls=%async_computation | async-start | bytes 4718592 | tf_op jit(solution)/shard_map/psum | solution.py:146
  65.4 3.7 %copy-start.4 = (bf16[768,1536]{1,0:T(8,128)(2,1)S(1)}, bf16[768,1536]{1,0:T(8,128)(2,1)}, u32[]{:S(2)}) copy-start(bf16[768,1536]{1,0:T(8,128)(2,1)} %param.12) | copy-start | bytes 7077892
  69.0 0.7 copy-start.8
  69.0 78.9 %all-gather.2.cloned.1.call-start = ((), (), s32[]{:S(2)}) async-start(), calls=%async_computation.1 | async-start | bytes 2654208 | tf_op jit(solution)/shard_map/all_gather | solution.py:149
  69.7 52.6 %copy-start.9 = (f32[1536]{0:T(1024)S(1)}, f32[1536]{0:T(1024)}, u32[]{:S(2)}) copy-start(f32[1536]{0:T(1024)} %param.17) | copy-start | bytes 18436
  119.9 2.4 copy-start.5
  119.9 3.1 copy-start.7
  125.4 26.1 %copy-start.11 = (f32[1536]{0:T(1024)S(1)}, f32[1536]{0:T(1024)}, u32[]{:S(2)}) copy-start(f32[1536]{0:T(1024)} %param.18) | copy-start | bytes 18436
  125.5 125.6 %all-reduce.5.cloned.1.call-start = ((), (), s32[]{:S(2)}) async-start(), calls=%async_computation.2 | async-start | bytes 9437184 | tf_op jit(solution)/shard_map/psum | solution.py:155
  175.8 78.3 %copy-start.10 = (f32[1536]{0:T(1024)S(1)}, f32[1536]{0:T(1024)}, u32[]{:S(2)}) copy-start(f32[1536]{0:T(1024)} %param.19) | copy-start | bytes 18436
  254.1 2.2 copy-start.6
  319.7 0.7 copy-start.3
  325.3 0.6 copy-start.2
  325.9 24.7 %copy-start.1 = (bf16[3072,192]{0,1:T(8,128)(2,1)S(1)}, bf16[3072,192]{0,1:T(8,128)(2,1)}, u32[]{:S(2)}) copy-start(bf16[3072,192]{0,1:T(8,128)(2,1)} %param.20) | copy-start | bytes 3538948
Sparse Core Ops, SparseCore 0:
  69.1 50.7 all-reduce.2
  125.6 22.3 all-gather.1
  175.9 75.0 all-reduce.4
